TPU v7x, 512 devices: a whole 4x8x8 slice. The times are simulated.
512 devices in a mesh: pair: 64 (over z, y), split: 8 (over x, core).
Axes of the slice: x: 4, y: 8, z: 8, core: 2. Of those that a mesh axis runs over, the one named last changes fastest.
Arguments:
- descriptors: bfloat16 [64, 1024, 256], P('pair', 'split'), as said below
- points: bfloat16 [64, 3, 1024], P('pair', None, 'split'), may hold values from -6 to 6
- normals: bfloat16 [64, 3, 1024], P('pair', None, 'split'), may hold values from -6 to 6
- pair_list: int32 [1536, 2], replicated, may hold values from 0 to 63, as said below
- intersection: int32 [1536], P('pair'), may hold values from 256 to 1024
- pose_index: int32 [64], replicated, may hold values from 0 to 63, each once
Outputs:
- pair_cross: float32 [1536, 6, 6], P('pair')
- pose_hessian: float32 [64, 6, 6], P('pair')
- pose_gradient: float32 [64, 6], P('pair')
Inputs may be any that keep to these rules, and one draw needn't show every extreme that they name: `descriptors`: values stay within -24 to 24. `pair_list`: task k's source scan is scan k // 24. The owner of a scan s is s; a task's target has another owner than its source. Among the 24 tasks of one aligned block (tasks k // 24 alike), no owner holds the targets of more than 1 of them, and some owner holds exactly 1.
All inputs are finite; a program needn't handle non-finite values.
Results may differ from a plain program's by a relative error of at most 0.0003.
Values may be sent and summed in bfloat16 or wider, within the bound.
No kernel may reach another device: no remote copies, remote signals or barrier semaphores. Data moves between devices by JAX's collectives and lax.ppermute only.
A program may use at most 64 MiB of HBM per device.

v0:
```python
import jax
import jax.numpy as jnp
from jax import lax
from jax.sharding import PartitionSpec as P

task_group = 4


def rows_first(arrays, axis, dims):
    turned = [jnp.moveaxis(a, dim, 0) for a, dim in zip(arrays, dims)]
    both = jnp.concatenate([t.reshape(len(t), -1) for t in turned], axis=1)
    out, at, gathered = (lax.all_gather(both, axis, axis=0, tiled=True), 0, [])
    for t, dim in zip(turned, dims):
        share = out[:, at : at + t[0].size].reshape(-1, *t.shape[1:])
        gathered.append(jnp.moveaxis(share, 0, dim))
        at += t[0].size
    return tuple(gathered)


def sent_together(arrays, axis, split_dim, concat_dim, along):
    ends, at = ([], 0)
    for a in arrays[:-1]:
        at += a.shape[along]
        ends.append(at)
    both = jnp.concatenate(arrays, axis=along)
    return tuple(
        jnp.split(
            lax.all_to_all(both, axis, split_axis=split_dim, concat_axis=concat_dim, tiled=True),
            ends,
            axis=along,
        )
    )


def copy_for_each(shard, axis):
    copies = jnp.broadcast_to(shard, (lax.axis_size(axis), *shard.shape))
    return lax.all_to_all(copies, axis, split_axis=0, concat_axis=0, tiled=True)


def of_everyone(shard, axis):
    everything = copy_for_each(shard, axis)
    return jnp.sum(everything, axis=0)


def in_one(arrays, axis):
    ends = [0]
    for a in arrays:
        ends.append(ends[-1] + a.size)
    total = of_everyone(jnp.concatenate([a.ravel() for a in arrays]), axis)
    return tuple((total[b:e].reshape(a.shape) for a, b, e in zip(arrays, ends, ends[1:])))


def in_blocks(shard, dim, size):
    before, after = (shard.shape[:dim], shard.shape[dim + 1 :])
    return jnp.moveaxis(shard.reshape(*before, size, -1, *after), dim, 0)


def sent_and_summed(shard, axis, dim):
    pieces = in_blocks(shard, dim, lax.axis_size(axis))
    arrived = lax.all_to_all(pieces, axis, split_axis=0, concat_axis=0, tiled=True)
    return arrived.sum(axis=0)


def side_by_side(arrays, axis, dim, along):
    both = jnp.concatenate(arrays, axis=along)
    out, at, gathered = (sent_and_summed(both, axis, dim), 0, [])
    for a in arrays:
        gathered.append(lax.slice_in_dim(out, at, at + a.shape[along], axis=along))
        at += a.shape[along]
    return tuple(gathered)


def cross_second(left_vec, right_vec):
    return jnp.stack(
        [
            left_vec[:, 1] * right_vec[:, 2] - left_vec[:, 2] * right_vec[:, 1],
            left_vec[:, 2] * right_vec[:, 0] - left_vec[:, 0] * right_vec[:, 2],
            left_vec[:, 0] * right_vec[:, 1] - left_vec[:, 1] * right_vec[:, 0],
        ],
        axis=1,
    )


def assemble(softened, source, row_seen, counts, all_rows):
    highest = lax.Precision.HIGHEST
    matched = softened[:, :3]
    normal = softened[:, 3:]
    weight = (row_seen[None, :] < counts[:, None]).astype(jnp.float32)
    jacobian = jnp.concatenate(
        [cross_second(source, normal), normal, -cross_second(matched, normal), -normal], axis=1
    )
    residual = jnp.sum(normal * (source - matched), axis=1)
    weighted = jacobian * weight[:, None, :]
    hessian = jnp.einsum("tan,tbn->tab", weighted, jacobian, precision=highest) / all_rows
    gradient = jnp.einsum("tan,tn->ta", weighted, residual, precision=highest) / all_rows
    return (hessian, gradient)


def per_device(descriptors, points, normals, pair_list, intersection, pose_index):
    highest = lax.Precision.HIGHEST
    scan_dev, block_rows, feature_width = descriptors.shape
    split_count = lax.axis_size("split")
    own_index = lax.axis_index("pair")
    all_rows = block_rows * split_count
    task_count = intersection.shape[0]
    my_pairs = lax.dynamic_slice_in_dim(pair_list, own_index * task_count, task_count, 0)
    sources = my_pairs[:, 0] - own_index * scan_dev
    targets = my_pairs[:, 1]
    geometry = jnp.concatenate([points, normals], axis=1)
    source_desc, source_points = rows_first((descriptors, points), "split", (1, 2))
    target_desc, target_geometry = (
        lax.all_gather(descriptors, "pair", axis=0, tiled=True),
        lax.all_gather(geometry, "pair", axis=0, tiled=True),
    )
    score_scale = feature_width ** (-0.5)
    group_count = task_count // task_group

    def attend(indices):
        source_ids, tile_ids = indices
        queries = source_desc[source_ids]
        key_rows = target_desc[tile_ids]
        tile_geometry = target_geometry[tile_ids].astype(jnp.float32)
        scores = (
            jnp.einsum("gic,gjc->gij", queries, key_rows, preferred_element_type=jnp.float32)
            * score_scale
        )
        maxima = jnp.max(scores, axis=2)
        exponent = jnp.exp(scores - maxima[:, :, None])
        totals = jnp.sum(exponent, axis=2)
        moment = jnp.einsum("gij,gdj->gdi", exponent, tile_geometry, precision=highest)
        return (maxima, totals, moment)

    maxima, totals, moment = lax.map(
        attend, (sources.reshape(group_count, task_group), targets.reshape(group_count, task_group))
    )
    maxima = maxima.reshape(task_count, all_rows)
    totals = totals.reshape(task_count, all_rows)
    moment = moment.reshape(task_count, 6, all_rows)
    maxima_parts = maxima.reshape(task_count, 1, split_count, block_rows)
    totals_parts = totals.reshape(task_count, 1, split_count, block_rows)
    moment_parts = moment.reshape(task_count, 6, split_count, block_rows)
    maxima_parts, totals_parts, moment_parts = sent_together(
        (maxima_parts, totals_parts, moment_parts), "split", 2, 2, 1
    )
    highest_score = jnp.max(maxima_parts, axis=2)
    factor = jnp.exp(maxima_parts - highest_score[:, :, None, :])
    totals_row = jnp.sum(totals_parts * factor, axis=2)
    moment_row = jnp.sum(moment_parts * factor, axis=2)
    softened = moment_row / totals_row
    row_seen = lax.axis_index("split") * block_rows + jnp.arange(block_rows, dtype=jnp.int32)
    hessian, gradient = assemble(
        softened, points[sources].astype(jnp.float32), row_seen, intersection, all_rows
    )
    hessian, gradient = in_one((hessian, gradient), "split")
    pair_cross = hessian[:, :6, 6:]
    all_poses = pose_index.shape[0]
    source_pose = pose_index[my_pairs[:, 0]]
    target_pose = pose_index[targets]
    source_part = jnp.concatenate(
        [hessian[:, :6, :6].reshape(task_count, 36), gradient[:, :6]], axis=1
    )
    target_part = jnp.concatenate(
        [hessian[:, 6:, 6:].reshape(task_count, 36), gradient[:, 6:]], axis=1
    )
    pose_slots = jnp.arange(all_poses, dtype=jnp.int32)[:, None]
    onehot_source = (pose_slots == source_pose[None, :]).astype(jnp.float32)
    onehot_target = (pose_slots == target_pose[None, :]).astype(jnp.float32)
    pose_terms = (
        jnp.dot(onehot_source, source_part, precision=highest)
        + jnp.dot(onehot_target, target_part, precision=highest)
    ) / task_count
    hessian_rows, gradient_rows = side_by_side(
        (pose_terms[:, :36], pose_terms[:, 36:]), "pair", 0, 1
    )
    return (pair_cross, hessian_rows.reshape(-1, 6, 6), gradient_rows)


def solution(mesh):
    in_specs = (
        P("pair", "split", None),
        P("pair", None, "split"),
        P("pair", None, "split"),
        P(),
        P("pair"),
        P(),
    )
    out_specs = (P("pair", None, None), P("pair", None, None), P("pair", None))
    return jax.shard_map(
        per_device, mesh=mesh, in_specs=in_specs, out_specs=out_specs, check_vma=False
    )
```

profile of v0, /device:TPU:1, one launch (start us, length us, event | category | flops | bytes accessed | tf_op | source)
XLA Modules:
  0.0 201.5 jit_solution(15148078323751725928)
XLA Ops:
  7.2 0.7 all-gather.2.cloned.1.call-update
  8.1 0.8 copy.64
  9.0 0.7 pad_maximum_fusion.3
  9.7 46.9 %all_gather.11 = bf16[64,6,128]{2,1,0:T(8,128)(2,1)S(1)} all-gather(bf16[1,6,128]{2,1,0:T(8,128)(2,1)S(1)} %pad_maximum_fusion.3), channel_id=1, replica_groups=mesh['pair'=64,'split'=8] {'pair'}, dimensions={0}, use_global_device_ids=true | all-gather | bytes 99840 | tf_op jit(solution)/shard_map/all_gather | solution.py:113
  56.6 0.9 pad_maximum_fusion.1
  57.4 24.7 %all_gather.9 = bf16[1024,259]{1,0:T(8,128)(2,1)S(1)} all-gather(bf16[128,259]{1,0:T(8,128)(2,1)S(1)} %pad_maximum_fusion.1), channel_id=1, replica_groups=mesh['pair'=64,'split'=8] {'split'}, dimensions={0}, use_global_device_ids=true | all-gather | bytes 596736 | tf_op jit(solution)/shard_map/all_gather | solution.py:12
  82.1 17.0 %all-gather.2.cloned.1.call-done = bf16[64,128,256]{2,1,0:T(8,128)(2,1)} async-done(((bf16[1,128,256]{2,1,0:T(8,128)(2,1)}), bf16[64,128,256]{2,1,0:T(8,128)(2,1)}) %all-gather.2.cloned.1.call-update) | async-done | bytes 4194320 | tf_op jit(solution)/shard_map/all_gather | solution.py:112
  99.1 37.8 %while.15 = (s32[]{:T(128)}, f32[6,4,1024]{2,1,0:T(4,128)S(1)}, f32[6,4,1024]{2,1,0:T(4,128)S(1)}, f32[6,4,6,1024]{3,2,1,0:T(8,128)}, bf16[1,1024,256]{2,1,0:T(8...) while((s32[]{:T(128)}, f32[6,4,1024]{2,1,0:T(4,128)S(1)}, ...), condition=%wide.region_3.4_spmd.clone, body=%wide.region_0.3_spmd.clone.sunk | while | flops 309847040 | bytes 7887541 | solution.py:133
  99.2 2.7 %gather_fusion = bf16[4,128,256]{2,1,0:T(8,128)(2,1)S(1)} fusion(bf16[64,128,256]{2,1,0:T(8,128)(2,1)} %get-tuple-element.215, s32[1024]{0:T(1024)S(1)} %pad_clamp_fusion.4), kind=kCustom, calls=%fused_computation.clone.1 | custom fusion | bytes 524304 | tf_op jit(solution)/shard_map/while/body/eval_jaxpr/gather | solution.py:121
  101.9 0.8 bitcast_reduce_fusion.2
  102.8 0.6 gather_fusion.1
  103.3 1.7 fusion.60
  105.0 0.4 fusion.59
  105.5 2.8 %gather_fusion = bf16[4,128,256]{2,1,0:T(8,128)(2,1)S(1)} fusion(bf16[64,128,256]{2,1,0:T(8,128)(2,1)} %get-tuple-element.215, s32[1024]{0:T(1024)S(1)} %pad_clamp_fusion.4), kind=kCustom, calls=%fused_computation.clone.1 | custom fusion | bytes 524304 | tf_op jit(solution)/shard_map/while/body/eval_jaxpr/gather | solution.py:121
  108.2 0.8 bitcast_reduce_fusion.2
  109.1 0.6 gather_fusion.1
  109.6 1.7 fusion.60
  111.3 0.4 fusion.59
  111.8 2.8 %gather_fusion = bf16[4,128,256]{2,1,0:T(8,128)(2,1)S(1)} fusion(bf16[64,128,256]{2,1,0:T(8,128)(2,1)} %get-tuple-element.215, s32[1024]{0:T(1024)S(1)} %pad_clamp_fusion.4), kind=kCustom, calls=%fused_computation.clone.1 | custom fusion | bytes 524304 | tf_op jit(solution)/shard_map/while/body/eval_jaxpr/gather | solution.py:121
  114.5 0.8 bitcast_reduce_fusion.2
  115.4 0.6 gather_fusion.1
  115.9 1.7 fusion.60
  117.6 0.4 fusion.59
  118.1 2.8 %gather_fusion = bf16[4,128,256]{2,1,0:T(8,128)(2,1)S(1)} fusion(bf16[64,128,256]{2,1,0:T(8,128)(2,1)} %get-tuple-element.215, s32[1024]{0:T(1024)S(1)} %pad_clamp_fusion.4), kind=kCustom, calls=%fused_computation.clone.1 | custom fusion | bytes 524304 | tf_op jit(solution)/shard_map/while/body/eval_jaxpr/gather | solution.py:121
  120.8 0.8 bitcast_reduce_fusion.2
  121.7 0.6 gather_fusion.1
  122.2 1.7 fusion.60
  123.9 0.4 fusion.59
  124.4 2.8 %gather_fusion = bf16[4,128,256]{2,1,0:T(8,128)(2,1)S(1)} fusion(bf16[64,128,256]{2,1,0:T(8,128)(2,1)} %get-tuple-element.215, s32[1024]{0:T(1024)S(1)} %pad_clamp_fusion.4), kind=kCustom, calls=%fused_computation.clone.1 | custom fusion | bytes 524304 | tf_op jit(solution)/shard_map/while/body/eval_jaxpr/gather | solution.py:121
  127.1 0.8 bitcast_reduce_fusion.2
  128.0 0.6 gather_fusion.1
  128.5 1.7 fusion.60
  130.2 0.4 fusion.59
  130.7 2.8 %gather_fusion = bf16[4,128,256]{2,1,0:T(8,128)(2,1)S(1)} fusion(bf16[64,128,256]{2,1,0:T(8,128)(2,1)} %get-tuple-element.215, s32[1024]{0:T(1024)S(1)} %pad_clamp_fusion.4), kind=kCustom, calls=%fused_computation.clone.1 | custom fusion | bytes 524304 | tf_op jit(solution)/shard_map/while/body/eval_jaxpr/gather | solution.py:121
  133.4 0.8 bitcast_reduce_fusion.2
  134.3 0.6 gather_fusion.1
  134.9 1.7 fusion.60
  136.6 0.4 fusion.59
  137.0 1.3 reshape.208
  138.4 1.0 copy.66
  139.4 9.2 %all-to-all-start = ((f32[24,8,8,128]{3,0,1,2:T(8,128)}), f32[24,8,8,128]{3,0,1,2:T(8,128)S(1)}, u32[]{:S(2)}, u32[]{:S(2)}) async-start(f32[24,8,8,128]{3,0,1,2:T(8,128)} %copy.66), calls=%async_computation | async-start | bytes 1572864 | tf_op jit(solution)/shard_map/all_to_all | solution.py:28
  148.8 12.0 %all-to-all-done = f32[24,8,8,128]{3,0,1,2:T(8,128)S(1)} async-done(((f32[24,8,8,128]{3,0,1,2:T(8,128)}), f32[24,8,8,128]{3,0,1,2:T(8,128)S(1)}, u32[]{:S(2)}, u32[]{:S(2)}) %all-to-all-start) | async-done | bytes 786464 | tf_op jit(solution)/shard_map/all_to_all | solution.py:28
  161.1 0.5 convolution_multiply_fusion
  161.5 0.1 reshape.153
  161.7 0.4 fusion.20
  162.1 0.1 reshape.154
  162.2 0.7 broadcast_in_dim.20
  162.9 4.2 %all-to-all-start.1 = ((f32[8,1,3744]{2,1,0:T(1,128)}), f32[8,1,3744]{2,1,0:T(1,128)S(1)}, u32[]{:S(2)}, u32[]{:S(2)}) async-start(f32[8,1,3744]{2,1,0:T(1,128)} %broadcast_in_dim.20), calls=%async_computation.1 | async-start | bytes 245760 | tf_op jit(solution)/shard_map/all_to_all | solution.py:37
  167.2 0.7 gather_fusion.2
  167.9 0.7 gather_fusion.3
  168.6 3.8 %all-to-all-done.1 = f32[8,1,3744]{2,1,0:T(1,128)S(1)} async-done(((f32[8,1,3744]{2,1,0:T(1,128)}), f32[8,1,3744]{2,1,0:T(1,128)S(1)}, u32[]{:S(2)}, u32[]{:S(2)}) %all-to-all-start.1) | async-done | bytes 119840 | tf_op jit(solution)/shard_map/all_to_all | solution.py:37
  172.3 0.1 reduce_sum.59
  172.4 0.1 reshape.155
  172.6 0.1 fusion.42
  172.9 0.1 reshape.157
  173.1 0.1 reshape.210
  173.4 0.2 fusion.29
  173.6 0.2 fusion.18
  173.7 0.7 copy.75
  174.4 8.0 %all-to-all-start.2 = ((f32[64,1,42]{2,1,0:T(1,128)}), f32[64,1,42]{2,1,0:T(1,128)S(1)}, u32[]{:S(2)}, u32[]{:S(2)}) async-start(f32[64,1,42]{2,1,0:T(1,128)} %copy.75), calls=%async_computation.2 | async-start | bytes 65536 | tf_op jit(solution)/shard_map/all_to_all | solution.py:60
  182.5 0.7 copy.76
  183.2 10.1 %all-to-all-done.2 = f32[64,1,42]{2,1,0:T(1,128)S(1)} async-done(((f32[64,1,42]{2,1,0:T(1,128)}), f32[64,1,42]{2,1,0:T(1,128)S(1)}, u32[]{:S(2)}, u32[]{:S(2)}) %all-to-all-start.2) | async-done | bytes 10784 | tf_op jit(solution)/shard_map/all_to_all | solution.py:60
  193.4 0.6 slice.132
  194.0 0.7 reshape.211
  (64 shorter events, 1.5 us)
Async XLA Ops:
  7.2 0.8 copy-start
  7.2 92.0 %all-gather.2.cloned.1.call-start = ((), (), s32[]{:S(2)}) async-start(), calls=%async_computation.3 | async-start | bytes 4259840 | tf_op jit(solution)/shard_map/all_gather | solution.py:112
  138.3 10.3 %copy-start.2 = (bf16[1,3,128]{2,1,0:T(4,128)(2,1)S(1)}, bf16[1,3,128]{2,1,0:T(4,128)(2,1)}, u32[]{:S(2)}) copy-start(bf16[1,3,128]{2,1,0:T(4,128)(2,1)} %param.9) | copy-start | bytes 2308
  138.4 10.4 %copy-start.3 = (s32[24]{0:T(128)S(1)}, s32[24]{0:T(128)}, u32[]{:S(2)}) copy-start(s32[24]{0:T(128)} %param.12) | copy-start | bytes 292
  139.4 21.4 %all-to-all-start = ((f32[24,8,8,128]{3,0,1,2:T(8,128)}), f32[24,8,8,128]{3,0,1,2:T(8,128)S(1)}, u32[]{:S(2)}, u32[]{:S(2)}) async-start(f32[24,8,8,128]{3,0,1,2:T(8,128)} %copy.66), calls=%async_computation | async-start | bytes 1572864 | tf_op jit(solution)/shard_map/all_to_all | solution.py:28
  148.7 18.5 %copy-start.1 = (s32[64]{0:T(128)S(1)}, s32[64]{0:T(128)}, u32[]{:S(2)}) copy-start(s32[64]{0:T(128)} %param.13) | copy-start | bytes 772
  162.9 9.4 %all-to-all-start.1 = ((f32[8,1,3744]{2,1,0:T(1,128)}), f32[8,1,3744]{2,1,0:T(1,128)S(1)}, u32[]{:S(2)}, u32[]{:S(2)}) async-start(f32[8,1,3744]{2,1,0:T(1,128)} %broadcast_in_dim.20), calls=%async_computation.1 | async-start | bytes 245760 | tf_op jit(solution)/shard_map/all_to_all | solution.py:37
  174.4 18.9 %all-to-all-start.2 = ((f32[64,1,42]{2,1,0:T(1,128)}), f32[64,1,42]{2,1,0:T(1,128)S(1)}, u32[]{:S(2)}, u32[]{:S(2)}) async-start(f32[64,1,42]{2,1,0:T(1,128)} %copy.75), calls=%async_computation.2 | async-start | bytes 65536 | tf_op jit(solution)/shard_map/all_to_all | solution.py:60
Sparse Core Ops, SparseCore 0:
  11.1 88.0 all-gather.1
where the time goes:
time: 202 us
  blocking collectives  71.6 us (35%)
  waiting for transfers between devices  43.6 us (22%)
  local copies, waits for them, and re-layouts  29.3 us (15%)
  starting transfers between devices  21.5 us (11%)
  matrix products  16.4 us (8%)
  between operations  14.4 us (7%)
  other arithmetic  4.44 us (2%)
    all_gather x1, blocking collectives, per_device(): lax.all_gather(geometry, 'pair', axis=0, tiled=True)  46.9 us
    all_gather x1, blocking collectives, rows_first(): out, at, gathered = (lax.all_gather(both, axis, axis=0, tiled=True), 0, [])  24.7 us
    all_gather x1, waiting for transfers between devices, per_device(): lax.all_gather(descriptors, 'pair', axis=0, tiled=True)  17 us
    gather x6, local copies, waits for them, and re-layouts, attend(): key_rows = target_desc[tile_ids]  16.5 us
    all_to_all x1, waiting for transfers between devices, sent_together(): lax.all_to_all(both, axis, split_axis=split_dim, concat_axis=concat_dim,...  12 us
    dot_general x6, matrix products, attend(): jnp.einsum('gij,gdj->gdi', exponent, tile_geometry, precision=highest)  10.2 us
    all_to_all x1, waiting for transfers between devices, sent_and_summed(): lax.all_to_all(pieces, axis, split_axis=0, concat_axis=0, tiled=True)  10.1 us
    all_to_all x1, starting transfers between devices, sent_together(): lax.all_to_all(both, axis, split_axis=split_dim, concat_axis=concat_dim,...  9.23 us
  transfers between devices with their start and end apart: 4, of which 4 were waited for; matrix products, arithmetic and copies ran while one was open for 2% of the time, Pallas kernels for 0%

commit v1 on v0

--- a/solution.py
+++ b/solution.py
@@ -4,6 +4,18 @@
 from jax.sharding import PartitionSpec as P
 
 task_group = 4
+
+
+def gather_by_bits(x, axis, dim):
+    ways, here, turn = (lax.axis_size(axis), lax.axis_index(axis), x.shape[dim])
+    line, have = (x, 1)
+    while have < ways:
+        line = jnp.concatenate(
+            [line, lax.ppermute(line, axis, [(d, (d - have) % ways) for d in range(ways)])],
+            axis=dim,
+        )
+        have = 2 * have
+    return jnp.roll(line, here * turn, axis=dim)
 
 
 def rows_first(arrays, axis, dims):
@@ -110,7 +122,7 @@
     source_desc, source_points = rows_first((descriptors, points), "split", (1, 2))
     target_desc, target_geometry = (
         lax.all_gather(descriptors, "pair", axis=0, tiled=True),
-        lax.all_gather(geometry, "pair", axis=0, tiled=True),
+        gather_by_bits(geometry, "pair", 0),
     )
     score_scale = feature_width ** (-0.5)
     group_count = task_count // task_group

time: 202 us -> 203 us (level)
  blocking collectives: 71.6 us -> 14.5 us
  starting transfers between devices: 21.5 us -> 51 us
  waiting for transfers between devices: 43.6 us -> 71 us
    all_gather x1 -> x0, blocking collectives: 46.9 us -> none  [per_device(): lax.all_gather(geometry, 'pair', axis=0, tiled=True)]
    ppermute x0 -> x6, starting transfers between devices: none -> 30.3 us  [gather_by_bits(): lax.ppermute(line, axis, [(d, (d - have) % ways) for d in range(ways)])]
    ppermute x0 -> x6, waiting for transfers between devices: none -> 16.3 us  [gather_by_bits(): lax.ppermute(line, axis, [(d, (d - have) % ways) for d in range(ways)])]
    all_gather x1, waiting for transfers between devices: 17 us -> 28 us  [per_device(): lax.all_gather(descriptors, 'pair', axis=0, tiled=True)]
    all_gather x1, blocking collectives: 24.7 us -> 14.5 us  [rows_first(): out, at, gathered = (lax.all_gather(both, axis, axis=0, tiled=True), 0, [])]
  transfers between devices with their start and end apart: 4 -> 10, of which waited for: 4 -> 9; matrix products, arithmetic and copies ran while one was open for 2% -> 2% of each run, Pallas kernels for 0% -> 0%
where the time goes in v1:
time: 203 us; the launch traced here: 202 us
  waiting for transfers between devices  71 us (35%)
  starting transfers between devices  51 us (25%)
  local copies, waits for them, and re-layouts  29.5 us (15%)
  matrix products  16.5 us (8%)
  blocking collectives  14.5 us (7%)
  between operations  14.5 us (7%)
  other arithmetic  4.48 us (2%)
    ppermute x6, starting transfers between devices, gather_by_bits(): lax.ppermute(line, axis, [(d, (d - have) % ways) for d in range(ways)])  30.3 us
    all_gather x1, waiting for transfers between devices, per_device(): lax.all_gather(descriptors, 'pair', axis=0, tiled=True)  28 us
    gather x6, local copies, waits for them, and re-layouts, attend(): key_rows = target_desc[tile_ids]  16.5 us
    ppermute x6, waiting for transfers between devices, gather_by_bits(): lax.ppermute(line, axis, [(d, (d - have) % ways) for d in range(ways)])  16.3 us
    all_gather x1, blocking collectives, rows_first(): out, at, gathered = (lax.all_gather(both, axis, axis=0, tiled=True), 0, [])  14.5 us
    all_to_all x1, waiting for transfers between devices, sent_together(): lax.all_to_all(both, axis, split_axis=split_dim, concat_axis=concat_dim,...  12 us
    dot_general x6, matrix products, attend(): jnp.einsum('gij,gdj->gdi', exponent, tile_geometry, precision=highest)  10.3 us
    all_to_all x1, waiting for transfers between devices, sent_and_summed(): lax.all_to_all(pieces, axis, split_axis=0, concat_axis=0, tiled=True)  10.2 us
  transfers between devices with their start and end apart: 10, of which 9 were waited for; matrix products, arithmetic and copies ran while one was open for 2% of the time, Pallas kernels for 0%

profile of v1, /device:TPU:1, one launch (start us, length us, event | category | flops | bytes accessed | tf_op | source)
XLA Modules:
  0.0 201.7 jit_solution(2899176254808171923)
XLA Ops:
  7.2 0.7 all-gather.2.cloned.1.call-update
  7.9 0.7 constant_dynamic-update-slice_fusion.10
  8.6 14.4 %collective-permute-start = (bf16[1,6,128]{2,1,0:T(8,128)(2,1)S(1)}, bf16[1,6,128]{2,1,0:T(8,128)(2,1)S(1)}, u32[]{:S(2)}, u32[]{:S(2)}) collective-permute-start(bf16[1,6,128]{2,1,0:T(8,128)(2,1)S(1)} %get-tuple-element.144), channel_id=1, source_target_pairs={{0,504},{8,0},{16,8},{24,16},{32,24},{40,32},{48,40},{56,48},{64,5... | collective-permute-start | bytes 4616 | tf_op jit(solution)/shard_map/ppermute | solution.py:14
  23.0 0.8 copy.64
  23.8 0.9 pad_maximum_fusion.1
  24.7 14.5 %all_gather.6 = bf16[1024,259]{1,0:T(8,128)(2,1)S(1)} all-gather(bf16[128,259]{1,0:T(8,128)(2,1)S(1)} %pad_maximum_fusion.1), channel_id=1, replica_groups=mesh['pair'=64,'split'=8] {'split'}, dimensions={0}, use_global_device_ids=true | all-gather | bytes 596736 | tf_op jit(solution)/shard_map/all_gather | solution.py:24
  39.3 3.8 %collective-permute-start.1 = (bf16[2,6,128]{2,1,0:T(8,128)(2,1)S(1)}, bf16[2,6,128]{2,1,0:T(8,128)(2,1)S(1)}, u32[]{:S(2)}, u32[]{:S(2)}) collective-permute-start(bf16[2,6,128]{2,1,0:T(8,128)(2,1)S(1)} %pad_maximum_fusion.5), channel_id=1, source_target_pairs={{0,496},{8,504},{16,0},{24,8},{32,16},{40,24},{48,32},{56,40},{64,... | collective-permute-start | bytes 9224 | tf_op jit(solution)/shard_map/ppermute | solution.py:14
  43.1 1.5 collective-permute-done.1
  44.6 4.8 %collective-permute-start.2 = (bf16[4,6,128]{2,1,0:T(8,128)(2,1)S(1)}, bf16[4,6,128]{2,1,0:T(8,128)(2,1)S(1)}, u32[]{:S(2)}, u32[]{:S(2)}) collective-permute-start(bf16[4,6,128]{2,1,0:T(8,128)(2,1)S(1)} %pad_maximum_fusion.4), channel_id=1, source_target_pairs={{0,480},{8,488},{16,496},{24,504},{32,0},{40,8},{48,16},{56,24},{6... | collective-permute-start | bytes 18440 | tf_op jit(solution)/shard_map/ppermute | solution.py:14
  49.4 3.5 %collective-permute-done.2 = bf16[4,6,128]{2,1,0:T(8,128)(2,1)S(1)} collective-permute-done((bf16[4,6,128]{2,1,0:T(8,128)(2,1)S(1)}, bf16[4,6,128]{2,1,0:T(8,128)(2,1)S(1)}, u32[]{:S(2)}, u32[]{:S(2)}) %collective-permute-start.2) | collective-permute-done | bytes 6176 | tf_op jit(solution)/shard_map/ppermute | solution.py:14
  52.9 2.1 %collective-permute-start.3 = (bf16[8,6,128]{2,1,0:T(8,128)(2,1)S(1)}, bf16[8,6,128]{2,1,0:T(8,128)(2,1)S(1)}, u32[]{:S(2)}, u32[]{:S(2)}) collective-permute-start(bf16[8,6,128]{2,1,0:T(8,128)(2,1)S(1)} %pad_maximum_fusion.2), channel_id=1, source_target_pairs={{0,448},{8,456},{16,464},{24,472},{32,480},{40,488},{48,496},{56,5... | collective-permute-start | bytes 36872 | tf_op jit(solution)/shard_map/ppermute | solution.py:14
  55.1 2.3 %collective-permute-done.3 = bf16[8,6,128]{2,1,0:T(8,128)(2,1)S(1)} collective-permute-done((bf16[8,6,128]{2,1,0:T(8,128)(2,1)S(1)}, bf16[8,6,128]{2,1,0:T(8,128)(2,1)S(1)}, u32[]{:S(2)}, u32[]{:S(2)}) %collective-permute-start.3) | collective-permute-done | bytes 12320 | tf_op jit(solution)/shard_map/ppermute | solution.py:14
  57.4 2.6 %collective-permute-start.4 = (bf16[16,6,128]{2,1,0:T(8,128)(2,1)S(1)}, bf16[16,6,128]{2,1,0:T(8,128)(2,1)S(1)}, u32[]{:S(2)}, u32[]{:S(2)}) collective-permute-start(bf16[16,6,128]{2,1,0:T(8,128)(2,1)S(1)} %get-tuple-element.126), channel_id=1, source_target_pairs={{0,384},{8,392},{16,400},{24,408},{32,416},{40,424},{48,432},{56,4... | collective-permute-start | bytes 73736 | tf_op jit(solution)/shard_map/ppermute | solution.py:14
  60.1 2.9 %collective-permute-done.4 = bf16[16,6,128]{2,1,0:T(8,128)(2,1)S(1)} collective-permute-done((bf16[16,6,128]{2,1,0:T(8,128)(2,1)S(1)}, bf16[16,6,128]{2,1,0:T(8,128)(2,1)S(1)}, u32[]{:S(2)}, u32[]{:S(2)}) %collective-permute-start.4) | collective-permute-done | bytes 24608 | tf_op jit(solution)/shard_map/ppermute | solution.py:14
  63.0 2.7 %collective-permute-start.5 = (bf16[32,6,128]{2,1,0:T(8,128)(2,1)S(1)}, bf16[32,6,128]{2,1,0:T(8,128)(2,1)S(1)}, u32[]{:S(2)}, u32[]{:S(2)}) collective-permute-start(bf16[32,6,128]{2,1,0:T(8,128)(2,1)S(1)} %get-tuple-element.122), channel_id=1, source_target_pairs={{0,256},{8,264},{16,272},{24,280},{32,288},{40,296},{48,304},{56,3... | collective-permute-start | bytes 147464 | tf_op jit(solution)/shard_map/ppermute | solution.py:14
  65.9 6.1 %collective-permute-done.5 = bf16[32,6,128]{2,1,0:T(8,128)(2,1)S(1)} collective-permute-done((bf16[32,6,128]{2,1,0:T(8,128)(2,1)S(1)}, bf16[32,6,128]{2,1,0:T(8,128)(2,1)S(1)}, u32[]{:S(2)}, u32[]{:S(2)}) %collective-permute-start.5) | collective-permute-done | bytes 49184 | tf_op jit(solution)/shard_map/ppermute | solution.py:14
  72.1 28.0 %all-gather.2.cloned.1.call-done = bf16[64,128,256]{2,1,0:T(8,128)(2,1)} async-done(((bf16[1,128,256]{2,1,0:T(8,128)(2,1)}), bf16[64,128,256]{2,1,0:T(8,128)(2,1)}) %all-gather.2.cloned.1.call-update) | async-done | bytes 4194320 | tf_op jit(solution)/shard_map/all_gather | solution.py:124
  100.1 37.9 %while.15 = (s32[]{:T(128)}, f32[6,4,1024]{2,1,0:T(4,128)S(1)}, f32[6,4,1024]{2,1,0:T(4,128)S(1)}, f32[6,4,6,1024]{3,2,1,0:T(8,128)}, bf16[1,1024,256]{2,1,0:T(8...) while((s32[]{:T(128)}, f32[6,4,1024]{2,1,0:T(4,128)S(1)}, ...), condition=%wide.region_3.4_spmd.clone, body=%wide.region_0.3_spmd.clone.sunk | while | flops 309847040 | bytes 7887541 | solution.py:145
  100.1 2.7 %gather_fusion = bf16[4,128,256]{2,1,0:T(8,128)(2,1)S(1)} fusion(bf16[64,128,256]{2,1,0:T(8,128)(2,1)} %get-tuple-element.233, s32[1024]{0:T(1024)S(1)} %pad_clamp_fusion.4), kind=kCustom, calls=%fused_computation.clone.1 | custom fusion | bytes 524304 | tf_op jit(solution)/shard_map/while/body/eval_jaxpr/gather | solution.py:133
  102.9 0.8 bitcast_reduce_fusion.2
  103.7 0.6 gather_fusion.1
  104.3 1.7 fusion.59
  106.0 0.4 fusion.58
  106.4 2.8 %gather_fusion = bf16[4,128,256]{2,1,0:T(8,128)(2,1)S(1)} fusion(bf16[64,128,256]{2,1,0:T(8,128)(2,1)} %get-tuple-element.233, s32[1024]{0:T(1024)S(1)} %pad_clamp_fusion.4), kind=kCustom, calls=%fused_computation.clone.1 | custom fusion | bytes 524304 | tf_op jit(solution)/shard_map/while/body/eval_jaxpr/gather | solution.py:133
  109.2 0.8 bitcast_reduce_fusion.2
  110.0 0.6 gather_fusion.1
  110.6 1.7 fusion.59
  112.3 0.4 fusion.58
  112.8 2.8 %gather_fusion = bf16[4,128,256]{2,1,0:T(8,128)(2,1)S(1)} fusion(bf16[64,128,256]{2,1,0:T(8,128)(2,1)} %get-tuple-element.233, s32[1024]{0:T(1024)S(1)} %pad_clamp_fusion.4), kind=kCustom, calls=%fused_computation.clone.1 | custom fusion | bytes 524304 | tf_op jit(solution)/shard_map/while/body/eval_jaxpr/gather | solution.py:133
  115.5 0.8 bitcast_reduce_fusion.2
  116.4 0.6 gather_fusion.1
  116.9 1.7 fusion.59
  118.6 0.4 fusion.58
  119.1 2.8 %gather_fusion = bf16[4,128,256]{2,1,0:T(8,128)(2,1)S(1)} fusion(bf16[64,128,256]{2,1,0:T(8,128)(2,1)} %get-tuple-element.233, s32[1024]{0:T(1024)S(1)} %pad_clamp_fusion.4), kind=kCustom, calls=%fused_computation.clone.1 | custom fusion | bytes 524304 | tf_op jit(solution)/shard_map/while/body/eval_jaxpr/gather | solution.py:133
  121.8 0.8 bitcast_reduce_fusion.2
  122.7 0.6 gather_fusion.1
  123.2 1.7 fusion.59
  125.0 0.4 fusion.58
  125.4 2.8 %gather_fusion = bf16[4,128,256]{2,1,0:T(8,128)(2,1)S(1)} fusion(bf16[64,128,256]{2,1,0:T(8,128)(2,1)} %get-tuple-element.233, s32[1024]{0:T(1024)S(1)} %pad_clamp_fusion.4), kind=kCustom, calls=%fused_computation.clone.1 | custom fusion | bytes 524304 | tf_op jit(solution)/shard_map/while/body/eval_jaxpr/gather | solution.py:133
  128.2 0.8 bitcast_reduce_fusion.2
  129.0 0.6 gather_fusion.1
  129.6 1.7 fusion.59
  131.3 0.4 fusion.58
  131.7 2.8 %gather_fusion = bf16[4,128,256]{2,1,0:T(8,128)(2,1)S(1)} fusion(bf16[64,128,256]{2,1,0:T(8,128)(2,1)} %get-tuple-element.233, s32[1024]{0:T(1024)S(1)} %pad_clamp_fusion.4), kind=kCustom, calls=%fused_computation.clone.1 | custom fusion | bytes 524304 | tf_op jit(solution)/shard_map/while/body/eval_jaxpr/gather | solution.py:133
  134.5 0.8 bitcast_reduce_fusion.2
  135.3 0.6 gather_fusion.1
  135.9 1.7 fusion.59
  138.0 1.3 reshape.208
  139.4 1.0 copy.66
  140.5 8.9 %all-to-all-start = ((f32[24,8,8,128]{3,0,1,2:T(8,128)}), f32[24,8,8,128]{3,0,1,2:T(8,128)S(1)}, u32[]{:S(2)}, u32[]{:S(2)}) async-start(f32[24,8,8,128]{3,0,1,2:T(8,128)} %copy.66), calls=%async_computation | async-start | bytes 1572864 | tf_op jit(solution)/shard_map/all_to_all | solution.py:40
  149.5 12.0 %all-to-all-done = f32[24,8,8,128]{3,0,1,2:T(8,128)S(1)} async-done(((f32[24,8,8,128]{3,0,1,2:T(8,128)}), f32[24,8,8,128]{3,0,1,2:T(8,128)S(1)}, u32[]{:S(2)}, u32[]{:S(2)}) %all-to-all-start) | async-done | bytes 786464 | tf_op jit(solution)/shard_map/all_to_all | solution.py:40
  161.8 0.5 convolution_multiply_fusion
  162.4 0.4 fusion.20
  162.9 0.7 broadcast_in_dim.20
  163.6 4.2 %all-to-all-start.1 = ((f32[8,1,3744]{2,1,0:T(1,128)}), f32[8,1,3744]{2,1,0:T(1,128)S(1)}, u32[]{:S(2)}, u32[]{:S(2)}) async-start(f32[8,1,3744]{2,1,0:T(1,128)} %broadcast_in_dim.20), calls=%async_computation.1 | async-start | bytes 245760 | tf_op jit(solution)/shard_map/all_to_all | solution.py:49
  167.9 0.7 gather_fusion.2
  168.6 0.7 gather_fusion.3
  169.3 3.8 %all-to-all-done.1 = f32[8,1,3744]{2,1,0:T(1,128)S(1)} async-done(((f32[8,1,3744]{2,1,0:T(1,128)}), f32[8,1,3744]{2,1,0:T(1,128)S(1)}, u32[]{:S(2)}, u32[]{:S(2)}) %all-to-all-start.1) | async-done | bytes 119840 | tf_op jit(solution)/shard_map/all_to_all | solution.py:49
  174.5 0.7 copy.75
  175.1 7.5 %all-to-all-start.2 = ((f32[64,1,42]{2,1,0:T(1,128)}), f32[64,1,42]{2,1,0:T(1,128)S(1)}, u32[]{:S(2)}, u32[]{:S(2)}) async-start(f32[64,1,42]{2,1,0:T(1,128)} %copy.75), calls=%async_computation.2 | async-start | bytes 65536 | tf_op jit(solution)/shard_map/all_to_all | solution.py:72
  182.6 0.7 copy.76
  183.4 10.2 %all-to-all-done.2 = f32[64,1,42]{2,1,0:T(1,128)S(1)} async-done(((f32[64,1,42]{2,1,0:T(1,128)}), f32[64,1,42]{2,1,0:T(1,128)S(1)}, u32[]{:S(2)}, u32[]{:S(2)}) %all-to-all-start.2) | async-done | bytes 10784 | tf_op jit(solution)/shard_map/all_to_all | solution.py:72
  193.6 0.6 slice.132
  194.2 0.7 reshape.211
  (94 shorter events, 3.1 us)
Async XLA Ops:
  7.2 52.8 %copy-start = (s32[1536,2]{0,1:T(2,128)S(1)}, s32[1536,2]{0,1:T(2,128)}, u32[]{:S(2)}) copy-start(s32[1536,2]{0,1:T(2,128)} %param.11) | copy-start | bytes 36868
  7.2 32.1 %copy-start.3 = (bf16[1,3,128]{2,1,0:T(4,128)(2,1)S(1)}, bf16[1,3,128]{2,1,0:T(4,128)(2,1)}, u32[]{:S(2)}) copy-start(bf16[1,3,128]{2,1,0:T(4,128)(2,1)} %param.10) | copy-start | bytes 2308
  7.2 32.1 %copy-start.2 = (bf16[1,3,128]{2,1,0:T(4,128)(2,1)S(1)}, bf16[1,3,128]{2,1,0:T(4,128)(2,1)}, u32[]{:S(2)}) copy-start(bf16[1,3,128]{2,1,0:T(4,128)(2,1)} %param.9) | copy-start | bytes 2308
  7.2 92.9 %all-gather.2.cloned.1.call-start = ((), (), s32[]{:S(2)}) async-start(), calls=%async_computation.3 | async-start | bytes 4259840 | tf_op jit(solution)/shard_map/all_gather | solution.py:124
  8.6 30.6 %collective-permute-start = (bf16[1,6,128]{2,1,0:T(8,128)(2,1)S(1)}, bf16[1,6,128]{2,1,0:T(8,128)(2,1)S(1)}, u32[]{:S(2)}, u32[]{:S(2)}) collective-permute-start(bf16[1,6,128]{2,1,0:T(8,128)(2,1)S(1)} %get-tuple-element.144), channel_id=1, source_target_pairs={{0,504},{8,0},{16,8},{24,16},{32,24},{40,32},{48,40},{56,48},{64,5... | collective-permute-start | bytes 4616 | tf_op jit(solution)/shard_map/ppermute | solution.py:14
  39.3 5.3 %collective-permute-start.1 = (bf16[2,6,128]{2,1,0:T(8,128)(2,1)S(1)}, bf16[2,6,128]{2,1,0:T(8,128)(2,1)S(1)}, u32[]{:S(2)}, u32[]{:S(2)}) collective-permute-start(bf16[2,6,128]{2,1,0:T(8,128)(2,1)S(1)} %pad_maximum_fusion.5), channel_id=1, source_target_pairs={{0,496},{8,504},{16,0},{24,8},{32,16},{40,24},{48,32},{56,40},{64,... | collective-permute-start | bytes 9224 | tf_op jit(solution)/shard_map/ppermute | solution.py:14
  44.6 8.3 %collective-permute-start.2 = (bf16[4,6,128]{2,1,0:T(8,128)(2,1)S(1)}, bf16[4,6,128]{2,1,0:T(8,128)(2,1)S(1)}, u32[]{:S(2)}, u32[]{:S(2)}) collective-permute-start(bf16[4,6,128]{2,1,0:T(8,128)(2,1)S(1)} %pad_maximum_fusion.4), channel_id=1, source_target_pairs={{0,480},{8,488},{16,496},{24,504},{32,0},{40,8},{48,16},{56,24},{6... | collective-permute-start | bytes 18440 | tf_op jit(solution)/shard_map/ppermute | solution.py:14
  52.9 4.5 %collective-permute-start.3 = (bf16[8,6,128]{2,1,0:T(8,128)(2,1)S(1)}, bf16[8,6,128]{2,1,0:T(8,128)(2,1)S(1)}, u32[]{:S(2)}, u32[]{:S(2)}) collective-permute-start(bf16[8,6,128]{2,1,0:T(8,128)(2,1)S(1)} %pad_maximum_fusion.2), channel_id=1, source_target_pairs={{0,448},{8,456},{16,464},{24,472},{32,480},{40,488},{48,496},{56,5... | collective-permute-start | bytes 36872 | tf_op jit(solution)/shard_map/ppermute | solution.py:14
  57.4 5.6 %collective-permute-start.4 = (bf16[16,6,128]{2,1,0:T(8,128)(2,1)S(1)}, bf16[16,6,128]{2,1,0:T(8,128)(2,1)S(1)}, u32[]{:S(2)}, u32[]{:S(2)}) collective-permute-start(bf16[16,6,128]{2,1,0:T(8,128)(2,1)S(1)} %get-tuple-element.126), channel_id=1, source_target_pairs={{0,384},{8,392},{16,400},{24,408},{32,416},{40,424},{48,432},{56,4... | collective-permute-start | bytes 73736 | tf_op jit(solution)/shard_map/ppermute | solution.py:14
  63.0 8.9 %collective-permute-start.5 = (bf16[32,6,128]{2,1,0:T(8,128)(2,1)S(1)}, bf16[32,6,128]{2,1,0:T(8,128)(2,1)S(1)}, u32[]{:S(2)}, u32[]{:S(2)}) collective-permute-start(bf16[32,6,128]{2,1,0:T(8,128)(2,1)S(1)} %get-tuple-element.122), channel_id=1, source_target_pairs={{0,256},{8,264},{16,272},{24,280},{32,288},{40,296},{48,304},{56,3... | collective-permute-start | bytes 147464 | tf_op jit(solution)/shard_map/ppermute | solution.py:14
  139.4 10.0 %copy-start.4 = (s32[24]{0:T(128)S(1)}, s32[24]{0:T(128)}, u32[]{:S(2)}) copy-start(s32[24]{0:T(128)} %param.12) | copy-start | bytes 292
  140.5 21.1 %all-to-all-start = ((f32[24,8,8,128]{3,0,1,2:T(8,128)}), f32[24,8,8,128]{3,0,1,2:T(8,128)S(1)}, u32[]{:S(2)}, u32[]{:S(2)}) async-start(f32[24,8,8,128]{3,0,1,2:T(8,128)} %copy.66), calls=%async_computation | async-start | bytes 1572864 | tf_op jit(solution)/shard_map/all_to_all | solution.py:40
  149.4 18.5 %copy-start.1 = (s32[64]{0:T(128)S(1)}, s32[64]{0:T(128)}, u32[]{:S(2)}) copy-start(s32[64]{0:T(128)} %param.13) | copy-start | bytes 772
  163.6 9.4 %all-to-all-start.1 = ((f32[8,1,3744]{2,1,0:T(1,128)}), f32[8,1,3744]{2,1,0:T(1,128)S(1)}, u32[]{:S(2)}, u32[]{:S(2)}) async-start(f32[8,1,3744]{2,1,0:T(1,128)} %broadcast_in_dim.20), calls=%async_computation.1 | async-start | bytes 245760 | tf_op jit(solution)/shard_map/all_to_all | solution.py:49
  175.1 18.4 %all-to-all-start.2 = ((f32[64,1,42]{2,1,0:T(1,128)}), f32[64,1,42]{2,1,0:T(1,128)S(1)}, u32[]{:S(2)}, u32[]{:S(2)}) async-start(f32[64,1,42]{2,1,0:T(1,128)} %copy.75), calls=%async_computation.2 | async-start | bytes 65536 | tf_op jit(solution)/shard_map/all_to_all | solution.py:72
Sparse Core Ops, SparseCore 0:
  11.1 88.9 all-gather.1
